TPU v7x, 32 devices: a whole 2x2x4 slice. The times are simulated.
32 devices in a mesh: grp: 16 (over z, y, x), node: 2 (over core).
Axes of the slice: x: 2, y: 2, z: 4, core: 2. Of those that a mesh axis runs over, the one named last changes fastest.
Arguments:
- grad_out: bfloat16 [6144, 2048], P('grp', 'node'), may hold values from -12 to 12
- gate_prob: float32 [6144], P('grp'), may hold values from 0.05 to 1
- hidden: bfloat16 [6144, 7168], P('grp', 'node'), may hold values from -0.19921875 to 0.19921875
- w_down: bfloat16 [2048, 7168], P(None, 'node'), may hold values from -0.0625 to 0.0625
- slot_counts: int32 [16], P('grp'), may hold values from 0 to 384, as said below
Outputs:
- grad_hidden: bfloat16 [6144, 7168], P('grp', 'node')
- grad_weight: bfloat16 [2048, 7168], P('grp', 'node')
Inputs may be any that keep to these rules, and one draw needn't show every extreme that they name: `slot_counts`: each count is a multiple of 128; in every draw some group's count is 384.
All inputs are finite; a program needn't handle non-finite values.
Results may differ from a plain program's by a relative error of at most 0.0057.
Values may be sent and summed in bfloat16 or wider, within the bound.
A program may use at most 128 MiB of HBM per device.

v0:
```python
import functools

import jax
import jax.numpy as jnp
from jax import lax
from jax.experimental import pallas as pl
from jax.experimental.pallas import tpu as pltpu
from jax.sharding import PartitionSpec as P

MESH = pl.DeviceIdType.MESH
LANES = 128
AHEAD = 1
HOP = 2
F32, BF16 = jnp.float32, jnp.bfloat16


def added(a, b):
    return (a.astype(F32) + b.astype(F32)).astype(BF16)


def kernel(
    dims, s_ref, hid_any, w_ref, gh_ref, gw_ref,
    g, acc, rx1, rx2, up, dn, wbuf, hid_ref, zacc, zup, zdn, za, zb,
    gsend, grecv, send1, recv1, send2, recv2, usend, urecv, dsend, drecv, wsem,
    zusend, zurecv, zdsend, zdrecv, zsend1, zrecv1, zsend2, zrecv2, hsem,
):
    nodes, depth, chunks, zchunks = dims
    total_chunks = chunks + zchunks
    node = lax.axis_index("node")
    me = lax.axis_index("grp")
    mx, my, mz = me % 2, (me // 2) % 2, me // 4
    px, py = 1 - mx, 1 - my
    half = s_ref.shape[1]
    wide = 2 * LANES
    rows = acc.shape[5]
    last = depth - 1
    not_first, not_last = mz > 0, mz < last

    def grp_at(z, y, x):
        return {"grp": (z * 2 + y) * 2 + x}

    to_x, to_y = grp_at(mz, my, px), grp_at(mz, py, mx)
    to_up, to_down = {"grp": me + 4}, {"grp": me - 4}

    barrier = pltpu.get_barrier_semaphore()

    def greet(target):
        pl.semaphore_signal(barrier, inc=1, device_id=target, device_id_type=MESH)

    greet(to_x)
    greet(to_y)
    for off in range(1, nodes):
        greet({"node": (node + off) % nodes})

    @pl.when(not_first)
    def _():
        greet(to_down)

    @pl.when(not_last)
    def _():
        greet(to_up)

    def w_copy(c, slot):
        cols = pl.ds(pl.multiple_of(c * wide, wide), wide)
        return pltpu.make_async_copy(w_ref.at[:, cols], wbuf.at[slot], wsem.at[slot])

    fetch = pltpu.make_async_copy(hid_any, hid_ref, hsem)
    fetch.start()
    w_copy(0, 0).start()
    pl.semaphore_wait(
        barrier, 1 + nodes + not_first.astype(jnp.int32) + not_last.astype(jnp.int32)
    )

    def remote(src, dst, ssem, rsem, target):
        return pltpu.make_async_remote_copy(
            src_ref=src, dst_ref=dst, send_sem=ssem, recv_sem=rsem,
            device_id=target, device_id_type=MESH,
        )

    def exchange(off):
        target = {"node": (node + off) % nodes}
        return remote(s_ref, g.at[node], gsend.at[off], grecv.at[off], target)

    for off in range(1, nodes):
        exchange(off).start()
    g[node] = s_ref[...]
    for off in range(1, nodes):
        exchange(off).wait()
    fetch.wait()

    def first(kind, c):
        if kind == 0:
            src, target = acc.at[0, c, :, :, px], to_x
        else:
            src, target = acc.at[1, c, :, py], to_y
        return remote(src, rx1.at[kind, c], send1.at[kind, c], recv1.at[kind, c], target)

    def second(kind, c):
        if kind == 0:
            src, target = acc.at[0, c, :, py, mx], to_y
        else:
            src, target = acc.at[1, c, :, my, px], to_x
        return remote(src, rx2.at[kind, c], send2.at[kind, c], recv2.at[kind, c], target)

    def line(c, d, rising):
        src = acc.at[:, c, d, my, mx]
        if rising:
            return remote(src, up.at[c, d], usend.at[c, d], urecv.at[c, d], to_up)
        return remote(src, dn.at[c, d], dsend.at[c, d], drecv.at[c, d], to_down)


    def make_term(into, c, column):
        cols = pl.ds(pl.multiple_of(column * wide, wide), wide)
        units = hid_ref[:, cols]

        def one(z, carry):
            tall = 4 * rows
            start = pl.multiple_of((z * tall) % half, tall)
            part = g[(z * tall) // half, :, pl.ds(start, tall)]
            product = lax.dot_general(
                part, units, (((0,), (0,)), ((), ())), preferred_element_type=F32
            ).astype(BF16)
            product = product.reshape(2, 2, rows, wide)
            into[0, c, z] = product[..., :LANES]
            into[1, c, z] = product[..., LANES:]
            return carry

        lax.fori_loop(0, depth, one, 0)

    def make_hidden(c):
        slot = c % 2
        w_copy(c, slot).wait()

        @pl.when(c + 1 < total_chunks)
        def _():
            w_copy(c + 1, 1 - slot).start()

        total = jnp.dot(g[0], wbuf[slot, :half, :], preferred_element_type=F32)
        for i in range(1, nodes):
            total += jnp.dot(
                g[i], wbuf[slot, i * half : (i + 1) * half, :], preferred_element_type=F32
            )
        gh_ref[:, pl.ds(pl.multiple_of(c * wide, wide), wide)] = total.astype(BF16)

    def within(c, run, count=chunks):
        @pl.when((c >= 0) & (c < count))
        def _():
            run(c)

    def step_make(c):
        make_term(acc, c, c)
        first(0, c).start()
        first(1, c).start()

    def step_second(c):
        first(0, c).wait_recv()
        acc[0, c, :, :, mx] = added(acc[0, c, :, :, mx], rx1[0, c])
        second(0, c).start()
        first(1, c).wait_recv()
        acc[1, c, :, my] = added(acc[1, c, :, my], rx1[1, c])
        second(1, c).start()

    def step_column(c):
        for kind in range(2):
            second(kind, c).wait_recv()
            acc[kind, c, :, my, mx] = added(acc[kind, c, :, my, mx], rx2[kind, c])

        @pl.when(mz == 0)
        def _():
            for d in range(last, 0, -1):
                line(c, d, True).start()

        @pl.when(mz == last)
        def _():
            for d in range(last):
                line(c, d, False).start()

    def step_rise(c):
        for d in range(last, 0, -1):
            @pl.when(d >= mz)
            def _():
                line(c, d, True).wait_recv()

            @pl.when(d > mz)
            def _():
                acc[:, c, d, my, mx] = added(acc[:, c, d, my, mx], up[c, d])
                line(c, d, True).start()

    def step_fall(c):
        for d in range(last):
            @pl.when(d <= mz)
            def _():
                line(c, d, False).wait_recv()

            @pl.when(d < mz)
            def _():
                acc[:, c, d, my, mx] = added(acc[:, c, d, my, mx], dn[c, d])
                line(c, d, False).start()

    def step_final(c):
        def put(total):
            for kind in range(2):
                cols = pl.ds(pl.multiple_of(c * wide + kind * LANES, LANES), LANES)
                gw_ref[:, cols] = total[kind].astype(BF16)

        @pl.when(mz == 0)
        def _():
            put(acc[:, c, mz, my, mx].astype(F32) + dn[c, mz].astype(F32))

        @pl.when(mz == last)
        def _():
            put(acc[:, c, mz, my, mx].astype(F32) + up[c, mz].astype(F32))

        @pl.when(not_first & not_last)
        def _():
            put(
                acc[:, c, mz, my, mx].astype(F32)
                + up[c, mz].astype(F32)
                + dn[c, mz].astype(F32)
            )

    def zline(q, d, rising):
        src = zacc.at[:, q, d]
        if rising:
            return remote(src, zup.at[q, d], zusend.at[q, d], zurecv.at[q, d], to_up)
        return remote(src, zdn.at[q, d], zdsend.at[q, d], zdrecv.at[q, d], to_down)

    def zfirst(kind, q):
        if kind == 0:
            src, target = zacc.at[0, q, mz, :, px], to_x
        else:
            src, target = zacc.at[1, q, mz, py], to_y
        return remote(src, za.at[kind, q], zsend1.at[kind, q], zrecv1.at[kind, q], target)

    def zsecond(kind, q):
        if kind == 0:
            src, target = zacc.at[0, q, mz, py, mx], to_y
        else:
            src, target = zacc.at[1, q, mz, my, px], to_x
        return remote(src, zb.at[kind, q], zsend2.at[kind, q], zrecv2.at[kind, q], target)

    def zmake(t):
        @pl.when(t % last == 0)
        def _():
            make_term(zacc, t // last, chunks + t // last)

    def zrise(m):
        q, d = m // last, last - m % last

        @pl.when(not_first & (d >= mz))
        def _():
            zline(q, d, True).wait_recv()
            zacc[:, q, d] = added(zacc[:, q, d], zup[q, d])

        @pl.when(d > mz)
        def _():
            zline(q, d, True).start()

    def zfall(m):
        q, d = m // last, m % last

        @pl.when(not_last & (d <= mz))
        def _():
            zline(q, d, False).wait_recv()
            zacc[:, q, d] = added(zacc[:, q, d], zdn[q, d])

        @pl.when(d < mz)
        def _():
            zline(q, d, False).start()

    def every_last(m, run):
        @pl.when((m >= 0) & (m % last == 0) & (m < zchunks * last))
        def _():
            run(m // last)

    def zstep_first(q):
        zfirst(0, q).start()
        zfirst(1, q).start()

    def zstep_second(q):
        zfirst(0, q).wait_recv()
        zacc[0, q, mz, :, mx] = added(zacc[0, q, mz, :, mx], za[0, q])
        zsecond(0, q).start()
        zfirst(1, q).wait_recv()
        zacc[1, q, mz, my] = added(zacc[1, q, mz, my], za[1, q])
        zsecond(1, q).start()

    def zstep_final(q):
        for kind in range(2):
            zsecond(kind, q).wait_recv()
            cols = pl.ds(
                pl.multiple_of((chunks + q) * wide + kind * LANES, LANES), LANES
            )
            gw_ref[:, cols] = added(zacc[kind, q, mz, my, mx], zb[kind, q])

    def step(t, carry):
        within(t, step_make)
        within(t, zmake, zchunks * last)
        @pl.when(mz == 0)
        def _():
            within(t, zrise, zchunks * last)

        @pl.when(mz == last)
        def _():
            within(t, zfall, zchunks * last)

        within(t, make_hidden, total_chunks)
        within(t - AHEAD, step_second)

        @pl.when(not_first)
        def _():
            within(t - HOP * mz, zrise, zchunks * last)

        @pl.when(not_last)
        def _():
            within(t - HOP * (last - mz), zfall, zchunks * last)

        done = t - HOP * last
        every_last(done, zstep_first)
        every_last(done - 1, zstep_second)
        every_last(done - 2, zstep_final)
        column = t - AHEAD - 1
        within(column, step_column)

        @pl.when(not_first)
        def _():
            within(column - HOP * mz, step_rise)

        @pl.when(not_last)
        def _():
            within(column - HOP * (last - mz), step_fall)

        within(column - HOP * last, step_final)
        return carry

    steps = max(chunks + AHEAD + 1 + HOP * last, (zchunks - 1 + HOP) * last + 3, total_chunks)
    lax.fori_loop(0, steps, step, 0)

    def drain(c, carry):
        for kind in range(2):
            first(kind, c).wait_send()
            second(kind, c).wait_send()
        for d in range(depth):
            @pl.when(d > mz)
            def _():
                line(c, d, True).wait_send()

            @pl.when(d < mz)
            def _():
                line(c, d, False).wait_send()
        return carry

    lax.fori_loop(0, chunks, drain, 0)

    def zdrain(q, carry):
        for kind in range(2):
            zfirst(kind, q).wait_send()
            zsecond(kind, q).wait_send()
        for d in range(depth):
            @pl.when(d > mz)
            def _():
                zline(q, d, True).wait_send()

            @pl.when(d < mz)
            def _():
                zline(q, d, False).wait_send()
        return carry

    lax.fori_loop(0, zchunks, zdrain, 0)


def body(grad_out, gate_prob, hidden, w_down, slot_counts):
    slots, half = grad_out.shape
    nodes, groups = lax.axis_size("node"), lax.axis_size("grp")
    depth = groups // 4
    model = w_down.shape[0]
    rows = model // groups
    units = hidden.shape[1]
    wide = 2 * LANES
    total_chunks = -(-units // wide)
    zchunks = max(1, round(total_chunks * 3 / 14))
    chunks = total_chunks - zchunks
    extra = total_chunks * wide - units
    live = lax.iota(jnp.int32, slots) < slot_counts[0]
    scaled = (gate_prob[:, None] * grad_out.astype(F32)).astype(BF16)
    scaled = jnp.where(live[:, None], scaled, jnp.zeros_like(scaled))
    if extra:
        hidden = jnp.pad(hidden, ((0, 0), (0, extra)))
        w_down = jnp.pad(w_down, ((0, 0), (0, extra)))
    dma = pltpu.SemaphoreType.DMA
    vmem = pl.BlockSpec(memory_space=pltpu.VMEM)
    grad_hidden, grad_weight = pl.pallas_call(
        functools.partial(kernel, (nodes, depth, chunks, zchunks)),
        out_shape=(
            pltpu.VMEM((slots, total_chunks * wide), BF16),
            pltpu.VMEM((rows, total_chunks * wide), BF16),
        ),
        in_specs=[vmem] + [pl.BlockSpec(memory_space=pl.ANY)] * 2,
        out_specs=(vmem, vmem),
        scratch_shapes=[
            pltpu.VMEM((nodes, slots, half), BF16),
            pltpu.VMEM((2, chunks, depth, 2, 2, rows, LANES), BF16),
            pltpu.VMEM((2, chunks, depth, 2, rows, LANES), BF16),
            pltpu.VMEM((2, chunks, depth, rows, LANES), BF16),
            pltpu.VMEM((chunks, depth, 2, rows, LANES), BF16),
            pltpu.VMEM((chunks, depth, 2, rows, LANES), BF16),
            pltpu.VMEM((2, model, wide), BF16),
            pltpu.VMEM((slots, total_chunks * wide), BF16),
            pltpu.VMEM((2, zchunks, depth, 2, 2, rows, LANES), BF16),
            pltpu.VMEM((zchunks, depth, 2, 2, 2, rows, LANES), BF16),
            pltpu.VMEM((zchunks, depth, 2, 2, 2, rows, LANES), BF16),
            pltpu.VMEM((2, zchunks, 2, rows, LANES), BF16),
            pltpu.VMEM((2, zchunks, rows, LANES), BF16),
            dma((nodes,)),
            dma((nodes,)),
            dma((2, chunks)),
            dma((2, chunks)),
            dma((2, chunks)),
            dma((2, chunks)),
            dma((chunks, depth)),
            dma((chunks, depth)),
            dma((chunks, depth)),
            dma((chunks, depth)),
            dma((2,)),
            dma((zchunks, depth)),
            dma((zchunks, depth)),
            dma((zchunks, depth)),
            dma((zchunks, depth)),
            dma((2, zchunks)),
            dma((2, zchunks)),
            dma((2, zchunks)),
            dma((2, zchunks)),
            dma(()),
        ],
        compiler_params=pltpu.CompilerParams(
            collective_id=0, has_side_effects=True, vmem_limit_bytes=54 * 1024 * 1024
        ),
    )(scaled, hidden, w_down)
    return grad_hidden[:, :units], grad_weight[:, :units]


def solution(mesh):
    return jax.shard_map(
        body,
        mesh=mesh,
        in_specs=(P("grp", "node"), P("grp"), P("grp", "node"), P(None, "node"), P("grp")),
        out_specs=(P("grp", "node"), P("grp", "node")),
        check_vma=False,
    )
```

profile of v0, /device:TPU:0, one launch (start us, length us, event | category | flops | bytes accessed | tf_op | source)
XLA Modules:
  0.0 130.6 jit_solution(14720409145558489973)
XLA Ops:
  1.3 2.3 %fusion.s_ref = bf16[384,1024]{1,0:T(8,128)(2,1)} fusion(bf16[384,1024]{1,0:T(8,128)(2,1)} %param.5, f32[384]{0:T(512)} %param.6, pred[384]{0:T(512)(128)(4,1)S(1)} %iota_compare_fusion), kind=kLoop, calls=%fused_computation.1 | loop fusion | flops 1572864 | bytes 1574784 | tf_op jit(solution)/shard_map/jit(_where)/select_n | solution.py:386
  3.6 124.5 %shard_map.68 = (bf16[384,3584]{1,0:T(8,128)(2,1)S(1)}, bf16[128,3584]{1,0:T(8,128)(2,1)S(1)}) custom-call(bf16[384,1024]{1,0:T(8,128)(2,1)} %fusion.s_ref, bf16[384,3584]{1,0:T(8,128)(2,1)} %hid_any.1, bf16[2048,3584]{1,0:T(8,128)(2,1)} %w_ref.1), custom_call_target="tpu_custom_call" | custom-call | tf_op jit(solution)/shard_map/pallas_call | solution.py:392
  128.1 1.5 %copy.9 = bf16[384,3584]{1,0:T(8,128)(2,1)} copy(bf16[384,3584]{1,0:T(8,128)(2,1)S(1)} %get-tuple-element.2) | data formatting | bytes 5505024
  129.6 0.9 copy.10
  (1 shorter events, 0.0 us)
where the time goes:
time: 131 us
  Pallas kernels  125 us (95%)
  local copies, waits for them, and re-layouts  2.46 us (2%)
  other arithmetic  2.27 us (2%)
    pallas_call x1, Pallas kernels, body(): pl.pallas_call(functools.partial(kernel, (nodes, depth, chunks, zchunks))...  125 us

commit v1 on v0

v1 whole, which is shorter than its diff:
```python
import functools

import jax
import jax.numpy as jnp
from jax import lax
from jax.experimental import pallas as pl
from jax.experimental.pallas import tpu as pltpu
from jax.sharding import PartitionSpec as P

MESH = pl.DeviceIdType.MESH
LANES = 128
WIDE = 2 * LANES
AHEAD = 1
HOP = 2
F32, BF16 = jnp.float32, jnp.bfloat16


def added(*terms):
    total = terms[0].astype(F32)
    for term in terms[1:]:
        total += term.astype(F32)
    return total.astype(BF16)


def kernel(
    dims, go_any, gate_ref, count_ref, hid_any, w_ref, gh_ref, gw_ref,
    go, g, shalf, scat, hid, wbuf, acc, ry, up, dn,
    gosem, hsem, wsem, gsend, grecv, ssend, srecv, xsend, xrecv, fsend, frecv,
    hsend, hrecv, ysend, yrecv, usend, urecv, dsend, drecv,
):
    nodes, depth, chunks = dims
    node = lax.axis_index("node")
    me = lax.axis_index("grp")
    mx, my, mz = me % 2, (me // 2) % 2, me // 4
    px, py = 1 - mx, 1 - my
    slots, half = go.shape
    rows = acc.shape[3]
    near = shalf.shape[1]
    last = depth - 1
    not_first, not_last = mz > 0, mz < last

    to_x = {"grp": me + 1 - 2 * mx}
    to_y = {"grp": me + 2 - 4 * my}
    to_up, to_down = {"grp": me + 4}, {"grp": me - 4}

    barrier = pltpu.get_barrier_semaphore()

    def greet(target):
        pl.semaphore_signal(barrier, inc=1, device_id=target, device_id_type=MESH)

    greet(to_x)
    greet(to_y)
    for off in range(1, nodes):
        greet({"node": (node + off) % nodes})

    @pl.when(not_first)
    def _():
        greet(to_down)

    @pl.when(not_last)
    def _():
        greet(to_up)

    def columns(c):
        return pl.ds(pl.multiple_of(c * WIDE, WIDE), WIDE)

    def w_copy(c, slot):
        return pltpu.make_async_copy(w_ref.at[:, columns(c)], wbuf.at[slot], wsem.at[slot])

    own = pl.ds(0, slots)
    theirs = pl.ds(slots, slots)
    take_hidden = pltpu.make_async_copy(hid_any, hid.at[own], hsem)
    take_grad = pltpu.make_async_copy(go_any, go, gosem)
    take_grad.start()
    take_hidden.start()
    w_copy(0, 0).start()

    def remote(src, dst, ssem, rsem, target):
        return pltpu.make_async_remote_copy(
            src_ref=src, dst_ref=dst, send_sem=ssem, recv_sem=rsem,
            device_id=target, device_id_type=MESH,
        )

    def peer(off):
        return {"node": (node + off) % nodes}

    def swap_scaled(off):
        return remote(g.at[node], g.at[node], gsend.at[off], grecv.at[off], peer(off))

    def swap_turned(off):
        dst = scat.at[pl.ds(node * near, near), :, :, own]
        return remote(shalf.at[mx], dst, ssend.at[off], srecv.at[off], peer(off))

    def x_scaled(i):
        dst = scat.at[node * near + i, :, :, theirs]
        return remote(shalf.at[px, i], dst, xsend.at[i], xrecv.at[i], to_x)

    def forward(off, i):
        ref = scat.at[node * near + i, :, :, theirs]
        return remote(ref, ref, fsend.at[off, i], frecv.at[off, i], peer(off))

    def x_hidden(c):
        return remote(
            hid.at[own, columns(c)], hid.at[theirs, columns(c)],
            hsend.at[c], hrecv.at[c], to_x,
        )

    def y_copy(c, d):
        return remote(acc.at[c, d, py], ry.at[c, d], ysend.at[c, d], yrecv.at[c, d], to_y)

    def z_copy(c, d, rising, both):
        if both:
            pick = lambda ref: ref.at[c, d]
        else:
            pick = lambda ref: ref.at[c, d, my]
        if rising:
            return remote(pick(acc), pick(up), usend.at[c, d], urecv.at[c, d], to_up)
        return remote(pick(acc), pick(dn), dsend.at[c, d], drecv.at[c, d], to_down)

    def late(c):
        return c % 2 == 0

    def each_d(run, least=1):
        for k in range(last, least - 1, -1):
            @pl.when(mz + k <= last)
            def _():
                run(mz + k, k)

            @pl.when(mz - k >= 0)
            def _():
                run(mz - k, k)

    pl.semaphore_wait(
        barrier, 1 + nodes + not_first.astype(jnp.int32) + not_last.astype(jnp.int32)
    )
    take_hidden.wait()
    x_hidden(0).start()
    take_grad.wait()

    live = lax.broadcasted_iota(jnp.int32, (LANES, slots), 1) < count_ref[0]
    gate = jnp.broadcast_to(gate_ref[...].reshape(1, slots), (LANES, slots))
    gate = jnp.where(live, gate, 0.0).T
    for i in range(half // LANES):
        cols = pl.ds(i * LANES, LANES)
        scaled = (go[:, cols].astype(F32) * gate).astype(BF16)
        g[node, :, cols] = scaled
        turned = scaled.T
        for j in range(LANES // rows):
            b = i * (LANES // rows) + j
            shalf[b % 2, b // 4, (b // 2) % 2] = turned[j * rows : (j + 1) * rows]
    for i in range(near):
        x_scaled(i).start()
    for off in range(1, nodes):
        swap_turned(off).start()
        swap_scaled(off).start()
    lax.fori_loop(1, chunks, lambda c, carry: (x_hidden(c).start(), carry)[1], 0)
    for i in range(near):
        scat[node * near + i, :, :, :slots] = shalf[mx, i]
    for off in range(1, nodes):
        swap_scaled(off).wait_recv()

    def make_hidden(c):
        slot = c % 2
        w_copy(c, slot).wait()

        @pl.when(c + 1 < chunks)
        def _():
            w_copy(c + 1, 1 - slot).start()

        total = jnp.dot(g[0], wbuf[slot, :half, :], preferred_element_type=F32)
        for i in range(1, nodes):
            total += jnp.dot(
                g[i], wbuf[slot, i * half : (i + 1) * half, :], preferred_element_type=F32
            )
        gh_ref[:, columns(c)] = total.astype(BF16)

    def hidden_range(start, stop):
        lax.fori_loop(start, stop, lambda c, carry: (make_hidden(c), carry)[1], 0)

    done = 0
    for i in range(near):
        until = chunks * (i + 2) // (near + 2)
        hidden_range(done, until)
        done = until
        x_scaled(i).wait_recv()
        for off in range(1, nodes):
            forward(off, i).start()
    hidden_range(done, chunks)
    for off in range(1, nodes):
        swap_turned(off).wait_recv()
        for i in range(near):
            forward(off, i).wait_recv()

    def make(c):
        x_hidden(c).wait_recv()
        units = hid[:, columns(c)]

        def two(j, carry):
            part = scat[pl.ds(2 * j, 2)].reshape(4 * rows, 2 * slots)
            product = jnp.dot(part, units, preferred_element_type=F32).astype(BF16)
            acc[c, pl.ds(2 * j, 2)] = product.reshape(2, 2, rows, WIDE)
            return carry

        lax.fori_loop(0, depth // 2, two, 0)

        def send(d, k):
            if k > 1:
                y_copy(c, d).start()
            else:
                @pl.when(jnp.logical_not(late(c)))
                def _():
                    y_copy(c, d).start()

        each_d(send)

    def pass_on(c, rising):
        inside = not_first if rising else not_last
        into = up if rising else dn

        def single(d):
            y_copy(c, d).wait_recv()

            @pl.when(inside)
            def _():
                z_copy(c, d, rising, False).wait_recv()
                acc[c, d, my] = added(acc[c, d, my], ry[c, d], into[c, d, my])

            @pl.when(jnp.logical_not(inside))
            def _():
                acc[c, d, my] = added(acc[c, d, my], ry[c, d])

            z_copy(c, d, rising, False).start()

        def double(d):
            @pl.when(inside)
            def _():
                z_copy(c, d, rising, False).wait_recv()
                acc[c, d, my] = added(acc[c, d, my], into[c, d, my])

            z_copy(c, d, rising, True).start()

        for k in range(last, 0, -1):
            d = mz + k if rising else mz - k

            @pl.when((d <= last) if rising else (d >= 0))
            def _():
                if k > 1:
                    single(d)
                else:
                    @pl.when(late(c))
                    def _():
                        double(d)

                    @pl.when(jnp.logical_not(late(c)))
                    def _():
                        single(d)

    def settle(c):
        @pl.when(late(c))
        def _():
            @pl.when(not_first)
            def _():
                z_copy(c, mz, True, True).wait_recv()
                acc[c, mz] = added(acc[c, mz], up[c, mz])

            @pl.when(not_last)
            def _():
                z_copy(c, mz, False, True).wait_recv()
                acc[c, mz] = added(acc[c, mz], dn[c, mz])

        y_copy(c, mz).start()

    def finish(c):
        y_copy(c, mz).wait_recv()
        cols = columns(c)

        @pl.when(late(c))
        def _():
            gw_ref[:, cols] = added(acc[c, mz, my], ry[c, mz])

        @pl.when(jnp.logical_not(late(c)))
        def _():
            @pl.when(not_first)
            def _():
                z_copy(c, mz, True, False).wait_recv()

            @pl.when(not_last)
            def _():
                z_copy(c, mz, False, False).wait_recv()

            @pl.when(mz == 0)
            def _():
                gw_ref[:, cols] = added(acc[c, mz, my], ry[c, mz], dn[c, mz, my])

            @pl.when(mz == last)
            def _():
                gw_ref[:, cols] = added(acc[c, mz, my], ry[c, mz], up[c, mz, my])

            @pl.when(not_first & not_last)
            def _():
                gw_ref[:, cols] = added(
                    acc[c, mz, my], ry[c, mz], up[c, mz, my], dn[c, mz, my]
                )

    def within(c, run):
        @pl.when((c >= 0) & (c < chunks))
        def _():
            run(c)

    def step(t, carry):
        within(t, make)

        @pl.when(not_last)
        def _():
            within(t - AHEAD - HOP * mz, lambda c: pass_on(c, True))

        @pl.when(not_first)
        def _():
            within(t - AHEAD - HOP * (last - mz), lambda c: pass_on(c, False))

        within(t - AHEAD - HOP * last, settle)
        within(t - AHEAD - HOP * last - 1, finish)
        return carry

    lax.fori_loop(0, chunks + AHEAD + HOP * last + 1, step, 0)

    for off in range(1, nodes):
        swap_turned(off).wait_send()
        swap_scaled(off).wait_send()
        for i in range(near):
            forward(off, i).wait_send()
    for i in range(near):
        x_scaled(i).wait_send()

    def drain(c, carry):
        x_hidden(c).wait_send()
        y_copy(c, mz).wait_send()

        def one(d, k):
            if k > 1:
                y_copy(c, d).wait_send()
            else:
                @pl.when(jnp.logical_not(late(c)))
                def _():
                    y_copy(c, d).wait_send()

        each_d(one)
        for k in range(1, depth):
            for rising in (True, False):
                d = mz + k if rising else mz - k

                @pl.when((d <= last) if rising else (d >= 0))
                def _():
                    if k > 1:
                        z_copy(c, d, rising, False).wait_send()
                    else:
                        @pl.when(late(c))
                        def _():
                            z_copy(c, d, rising, True).wait_send()

                        @pl.when(jnp.logical_not(late(c)))
                        def _():
                            z_copy(c, d, rising, False).wait_send()
        return carry

    lax.fori_loop(0, chunks, drain, 0)


def body(grad_out, gate_prob, hidden, w_down, slot_counts):
    slots, half = grad_out.shape
    nodes, groups = lax.axis_size("node"), lax.axis_size("grp")
    depth = groups // 4
    near = depth // nodes
    model = w_down.shape[0]
    rows = model // groups
    units = hidden.shape[1]
    chunks = -(-units // WIDE)
    extra = chunks * WIDE - units
    if extra:
        hidden = jnp.pad(hidden, ((0, 0), (0, extra)))
        w_down = jnp.pad(w_down, ((0, 0), (0, extra)))
    dma = pltpu.SemaphoreType.DMA
    vmem = pl.BlockSpec(memory_space=pltpu.VMEM)
    smem = pl.BlockSpec(memory_space=pltpu.SMEM)
    anywhere = pl.BlockSpec(memory_space=pl.ANY)
    grad_hidden, grad_weight = pl.pallas_call(
        functools.partial(kernel, (nodes, depth, chunks)),
        out_shape=(
            pltpu.VMEM((slots, chunks * WIDE), BF16),
            pltpu.VMEM((rows, chunks * WIDE), BF16),
        ),
        in_specs=[anywhere, vmem, smem, anywhere, anywhere],
        out_specs=(vmem, vmem),
        scratch_shapes=[
            pltpu.VMEM((slots, half), BF16),
            pltpu.VMEM((nodes, slots, half), BF16),
            pltpu.VMEM((2, near, 2, rows, slots), BF16),
            pltpu.VMEM((depth, 2, rows, 2 * slots), BF16),
            pltpu.VMEM((2 * slots, chunks * WIDE), BF16),
            pltpu.VMEM((2, model, WIDE), BF16),
            pltpu.VMEM((chunks, depth, 2, rows, WIDE), BF16),
            pltpu.VMEM((chunks, depth, rows, WIDE), BF16),
            pltpu.VMEM((chunks, depth, 2, rows, WIDE), BF16),
            pltpu.VMEM((chunks, depth, 2, rows, WIDE), BF16),
            dma(()),
            dma(()),
            dma((2,)),
            dma((nodes,)),
            dma((nodes,)),
            dma((nodes,)),
            dma((nodes,)),
            dma((near,)),
            dma((near,)),
            dma((nodes, near)),
            dma((nodes, near)),
            dma((chunks,)),
            dma((chunks,)),
            dma((chunks, depth)),
            dma((chunks, depth)),
            dma((chunks, depth)),
            dma((chunks, depth)),
            dma((chunks, depth)),
            dma((chunks, depth)),
        ],
        compiler_params=pltpu.CompilerParams(
            collective_id=0, has_side_effects=True, vmem_limit_bytes=54 * 1024 * 1024
        ),
    )(grad_out, gate_prob, slot_counts, hidden, w_down)
    return grad_hidden[:, :units], grad_weight[:, :units]


def solution(mesh):
    return jax.shard_map(
        body,
        mesh=mesh,
        in_specs=(P("grp", "node"), P("grp"), P("grp", "node"), P(None, "node"), P("grp")),
        out_specs=(P("grp", "node"), P("grp", "node")),
        check_vma=False,
    )
```

time: 131 us -> 117 us (0.89)
  the two profiles are of different devices: /device:TPU:0 before, /device:TPU:16 now
where the time goes in v1:
time: 117 us; the launch traced here: 116 us
  Pallas kernels  112 us (96%)
  local copies, waits for them, and re-layouts  2.46 us (2%)
  between operations  1.29 us (1%)
    pallas_call x1, Pallas kernels, body(): pl.pallas_call(functools.partial(kernel, (nodes, depth, chunks)), out_sha...  112 us
    unnamed x2, local copies, waits for them, and re-layouts  2.46 us

profile of v1, /device:TPU:16, one launch (start us, length us, event | category | flops | bytes accessed | tf_op | source)
XLA Modules:
  0.0 116.0 jit_solution(5570636630540558661)
XLA Ops:
  1.3 112.2 %shard_map.68 = (bf16[384,3584]{1,0:T(8,128)(2,1)S(1)}, bf16[128,3584]{1,0:T(8,128)(2,1)S(1)}) custom-call(bf16[384,1024]{1,0:T(8,128)(2,1)} %go_any.1, f32[384]{0:T(512)} %gate_ref.1, s32[1]{0:T(128)S(6)} %copy.11.count_ref, bf16[384,3584]{1,0:T(8,128)(2,1)} %hid_any.1, bf16[2048,3584]{1,0:T(8,128)(2,1)} %w_ref.1), custom_call_target="tpu_custom_call" | custom-call | tf_op jit(solution)/shard_map/pallas_call | solution.py:386
  113.5 1.5 %copy.9 = bf16[384,3584]{1,0:T(8,128)(2,1)} copy(bf16[384,3584]{1,0:T(8,128)(2,1)S(1)} %get-tuple-element.2) | data formatting | bytes 5505024
  115.1 0.9 copy.10

commit v2 on v1

--- a/solution.py
+++ b/solution.py
@@ -11,7 +11,10 @@
 LANES = 128
 WIDE = 2 * LANES
 AHEAD = 1
-HOP = 2
+HOP = 1
+DEFER = 1
+NEAR = 2
+EARLY = 3
 F32, BF16 = jnp.float32, jnp.bfloat16
 
 
@@ -91,12 +94,16 @@
         dst = scat.at[pl.ds(node * near, near), :, :, own]
         return remote(shalf.at[mx], dst, ssend.at[off], srecv.at[off], peer(off))
 
+    def nth(owner, i):
+        return jnp.where(2 * owner < nodes, i, near - 1 - i)
+
     def x_scaled(i):
-        dst = scat.at[node * near + i, :, :, theirs]
-        return remote(shalf.at[px, i], dst, xsend.at[i], xrecv.at[i], to_x)
+        j = nth(node, i)
+        dst = scat.at[node * near + j, :, :, theirs]
+        return remote(shalf.at[px, j], dst, xsend.at[i], xrecv.at[i], to_x)
 
     def forward(off, i):
-        ref = scat.at[node * near + i, :, :, theirs]
+        ref = scat.at[node * near + nth(node, i), :, :, theirs]
         return remote(ref, ref, fsend.at[off, i], frecv.at[off, i], peer(off))
 
     def x_hidden(c):
@@ -118,7 +125,7 @@
         return remote(pick(acc), pick(dn), dsend.at[c, d], drecv.at[c, d], to_down)
 
     def late(c):
-        return c % 2 == 0
+        return (c % 2 == 1) & (c < chunks - 3)
 
     def each_d(run, least=1):
         for k in range(last, least - 1, -1):
@@ -177,19 +184,37 @@
     def hidden_range(start, stop):
         lax.fori_loop(start, stop, lambda c, carry: (make_hidden(c), carry)[1], 0)
 
+    def send(c, d):
+        k = jnp.abs(d - mz)
+
+        @pl.when((k > 1) | ((k == 1) & jnp.logical_not(late(c))))
+        def _():
+            y_copy(c, d).start()
+
+    def make_first(owner, i):
+        d = owner * near + nth(owner, i)
+        part = scat[d].reshape(2 * rows, 2 * slots)
+        product = jnp.dot(part, hid[:, :WIDE], preferred_element_type=F32).astype(BF16)
+        acc[0, d] = product.reshape(2, rows, WIDE)
+        send(0, d)
+
     done = 0
     for i in range(near):
-        until = chunks * (i + 2) // (near + 2)
+        until = chunks * (i + near) // (2 * near)
         hidden_range(done, until)
         done = until
+        if i == 0:
+            for off in range(1, nodes):
+                swap_turned(off).wait_recv()
         x_scaled(i).wait_recv()
         for off in range(1, nodes):
             forward(off, i).start()
-    hidden_range(done, chunks)
-    for off in range(1, nodes):
-        swap_turned(off).wait_recv()
-        for i in range(near):
+        if i == 0:
+            x_hidden(0).wait_recv()
+        make_first(node, i)
+        for off in range(1, nodes):
             forward(off, i).wait_recv()
+            make_first((node + nodes - off) % nodes, i)
 
     def make(c):
         x_hidden(c).wait_recv()
@@ -203,15 +228,17 @@
 
         lax.fori_loop(0, depth // 2, two, 0)
 
-        def send(d, k):
-            if k > 1:
-                y_copy(c, d).start()
-            else:
-                @pl.when(jnp.logical_not(late(c)))
-                def _():
-                    y_copy(c, d).start()
-
-        each_d(send)
+        @pl.when(late(c) & (c < EARLY))
+        def _():
+            @pl.when(mz == 0)
+            def _():
+                hand_over(c, True)
+
+            @pl.when(mz == last)
+            def _():
+                hand_over(c, False)
+
+        each_d(lambda d, k: send(c, d))
 
     def pass_on(c, rising):
         inside = not_first if rising else not_last
@@ -231,29 +258,32 @@
 
             z_copy(c, d, rising, False).start()
 
-        def double(d):
-            @pl.when(inside)
-            def _():
-                z_copy(c, d, rising, False).wait_recv()
-                acc[c, d, my] = added(acc[c, d, my], into[c, d, my])
-
+        for k in range(last, 1, -1):
+            d = mz + k if rising else mz - k
+
+            @pl.when((d <= last) if rising else (d >= 0))
+            def _():
+                single(d)
+
+    def hand_over(c, rising):
+        inside = not_first if rising else not_last
+        into = up if rising else dn
+        d = mz + 1 if rising else mz - 1
+
+        @pl.when(inside)
+        def _():
+            z_copy(c, d, rising, False).wait_recv()
+            acc[c, d, my] = added(acc[c, d, my], into[c, d, my])
+
+        @pl.when(late(c))
+        def _():
             z_copy(c, d, rising, True).start()
 
-        for k in range(last, 0, -1):
-            d = mz + k if rising else mz - k
-
-            @pl.when((d <= last) if rising else (d >= 0))
-            def _():
-                if k > 1:
-                    single(d)
-                else:
-                    @pl.when(late(c))
-                    def _():
-                        double(d)
-
-                    @pl.when(jnp.logical_not(late(c)))
-                    def _():
-                        single(d)
+        @pl.when(jnp.logical_not(late(c)))
+        def _():
+            y_copy(c, d).wait_recv()
+            acc[c, d, my] = added(acc[c, d, my], ry[c, d])
+            z_copy(c, d, rising, False).start()
 
     def settle(c):
         @pl.when(late(c))
@@ -268,7 +298,7 @@
                 z_copy(c, mz, False, True).wait_recv()
                 acc[c, mz] = added(acc[c, mz], dn[c, mz])
 
-        y_copy(c, mz).start()
+            y_copy(c, mz).start()
 
     def finish(c):
         y_copy(c, mz).wait_recv()
@@ -307,22 +337,49 @@
         def _():
             run(c)
 
+    settled = AHEAD + HOP * last + DEFER + 1
+
     def step(t, carry):
-        within(t, make)
+        @pl.when((t > 0) & (t < chunks))
+        def _():
+            make(t)
+
+        @pl.when(t + done < chunks)
+        def _():
+            make_hidden(t + done)
+
+        rise = t - AHEAD - HOP * mz
+        fall = t - AHEAD - HOP * (last - mz)
 
         @pl.when(not_last)
         def _():
-            within(t - AHEAD - HOP * mz, lambda c: pass_on(c, True))
+            within(rise, lambda c: pass_on(c, True))
 
         @pl.when(not_first)
         def _():
-            within(t - AHEAD - HOP * (last - mz), lambda c: pass_on(c, False))
-
-        within(t - AHEAD - HOP * last, settle)
-        within(t - AHEAD - HOP * last - 1, finish)
+            within(fall, lambda c: pass_on(c, False))
+
+        def early(c, inside):
+            return late(c) & (c < EARLY) & jnp.logical_not(inside)
+
+        @pl.when(not_last & jnp.logical_not(early(rise - DEFER, not_first)))
+        def _():
+            within(rise - DEFER, lambda c: hand_over(c, True))
+
+        @pl.when(not_first & jnp.logical_not(early(fall - DEFER, not_last)))
+        def _():
+            within(fall - DEFER, lambda c: hand_over(c, False))
+
+        within(t - settled, settle)
+
+        @pl.when((t >= NEAR) & (t < chunks + NEAR) & jnp.logical_not(late(t - NEAR)))
+        def _():
+            y_copy(t - NEAR, mz).start()
+
+        within(t - settled - 2, finish)
         return carry
 
-    lax.fori_loop(0, chunks + AHEAD + HOP * last + 1, step, 0)
+    lax.fori_loop(0, chunks + settled + 2, step, 0)
 
     for off in range(1, nodes):
         swap_turned(off).wait_send()

time: 117 us -> 106 us (0.906)
  the two profiles are of different devices: /device:TPU:16 before, /device:TPU:0 now
where the time goes in v2:
time: 106 us; the launch traced here: 105 us
  Pallas kernels  102 us (96%)
  local copies, waits for them, and re-layouts  2.46 us (2%)
  between operations  1.29 us (1%)
    pallas_call x1, Pallas kernels, body(): pl.pallas_call(functools.partial(kernel, (nodes, depth, chunks)), out_sha...  102 us
    unnamed x2, local copies, waits for them, and re-layouts  2.46 us

profile of v2, /device:TPU:0, one launch (start us, length us, event | category | flops | bytes accessed | tf_op | source)
XLA Modules:
  0.0 105.4 jit_solution(13886860065331702375)
XLA Ops:
  1.3 101.7 %shard_map.68 = (bf16[384,3584]{1,0:T(8,128)(2,1)S(1)}, bf16[128,3584]{1,0:T(8,128)(2,1)S(1)}) custom-call(bf16[384,1024]{1,0:T(8,128)(2,1)} %go_any.1, f32[384]{0:T(512)} %gate_ref.1, s32[1]{0:T(128)S(6)} %copy.11.count_ref, bf16[384,3584]{1,0:T(8,128)(2,1)} %hid_any.1, bf16[2048,3584]{1,0:T(8,128)(2,1)} %w_ref.1), custom_call_target="tpu_custom_call" | custom-call | tf_op jit(solution)/shard_map/pallas_call | solution.py:443
  102.9 1.5 %copy.9 = bf16[384,3584]{1,0:T(8,128)(2,1)} copy(bf16[384,3584]{1,0:T(8,128)(2,1)S(1)} %get-tuple-element.2) | data formatting | bytes 5505024
  104.5 0.9 copy.10

commit v3 on v2

--- a/solution.py
+++ b/solution.py
@@ -1,4 +1,5 @@
 import functools
+from types import SimpleNamespace
 
 import jax
 import jax.numpy as jnp
@@ -13,8 +14,8 @@
 AHEAD = 1
 HOP = 1
 DEFER = 1
-NEAR = 2
-EARLY = 3
+NEAR = 3
+LAST = 3
 F32, BF16 = jnp.float32, jnp.bfloat16
 
 
@@ -27,18 +28,20 @@
 
 def kernel(
     dims, go_any, gate_ref, count_ref, hid_any, w_ref, gh_ref, gw_ref,
-    go, g, shalf, scat, hid, wbuf, acc, ry, up, dn,
+    go, g, sall, scat, hid, wbuf, acc, ry, up, dn, qacc, qry, qup, qdn, qrx,
     gosem, hsem, wsem, gsend, grecv, ssend, srecv, xsend, xrecv, fsend, frecv,
     hsend, hrecv, ysend, yrecv, usend, urecv, dsend, drecv,
+    qysend, qyrecv, qusend, qurecv, qdsend, qdrecv, qxsend, qxrecv,
 ):
-    nodes, depth, chunks = dims
+    nodes, depth, total_chunks = dims
+    chunks = total_chunks - 1
     node = lax.axis_index("node")
     me = lax.axis_index("grp")
     mx, my, mz = me % 2, (me // 2) % 2, me // 4
     px, py = 1 - mx, 1 - my
     slots, half = go.shape
     rows = acc.shape[3]
-    near = shalf.shape[1]
+    near = depth // nodes
     last = depth - 1
     not_first, not_last = mz > 0, mz < last
 
@@ -91,16 +94,16 @@
         return remote(g.at[node], g.at[node], gsend.at[off], grecv.at[off], peer(off))
 
     def swap_turned(off):
-        dst = scat.at[pl.ds(node * near, near), :, :, own]
-        return remote(shalf.at[mx], dst, ssend.at[off], srecv.at[off], peer(off))
+        ref = sall.at[pl.ds(node * near, near)]
+        return remote(ref, ref, ssend.at[off], srecv.at[off], peer(off))
 
     def nth(owner, i):
         return jnp.where(2 * owner < nodes, i, near - 1 - i)
 
     def x_scaled(i):
-        j = nth(node, i)
-        dst = scat.at[node * near + j, :, :, theirs]
-        return remote(shalf.at[px, j], dst, xsend.at[i], xrecv.at[i], to_x)
+        d = node * near + nth(node, i)
+        dst = scat.at[d, :, :, theirs]
+        return remote(sall.at[d, :, px], dst, xsend.at[i], xrecv.at[i], to_x)
 
     def forward(off, i):
         ref = scat.at[node * near + nth(node, i), :, :, theirs]
@@ -112,20 +115,35 @@
             hsend.at[c], hrecv.at[c], to_x,
         )
 
-    def y_copy(c, d):
-        return remote(acc.at[c, d, py], ry.at[c, d], ysend.at[c, d], yrecv.at[c, d], to_y)
-
-    def z_copy(c, d, rising, both):
+    def late(c):
+        return (c % 2 == 1) & (c > 2) & (c < chunks - 3)
+
+    main = SimpleNamespace(
+        acc=acc, ry=ry, up=up, dn=dn, late=late, ysend=ysend, yrecv=yrecv,
+        usend=usend, urecv=urecv, dsend=dsend, drecv=drecv,
+    )
+    lone = SimpleNamespace(
+        acc=qacc, ry=qry, up=qup, dn=qdn, late=lambda c: c < 0, ysend=qysend, yrecv=qyrecv,
+        usend=qusend, urecv=qurecv, dsend=qdsend, drecv=qdrecv,
+    )
+
+    def y_copy(f, c, d):
+        return remote(
+            f.acc.at[c, d, py], f.ry.at[c, d], f.ysend.at[c, d], f.yrecv.at[c, d], to_y
+        )
+
+    def z_copy(f, c, d, rising, both):
         if both:
             pick = lambda ref: ref.at[c, d]
         else:
             pick = lambda ref: ref.at[c, d, my]
         if rising:
-            return remote(pick(acc), pick(up), usend.at[c, d], urecv.at[c, d], to_up)
-        return remote(pick(acc), pick(dn), dsend.at[c, d], drecv.at[c, d], to_down)
-
-    def late(c):
-        return (c % 2 == 1) & (c < chunks - 3)
+            return remote(
+                pick(f.acc), pick(f.up), f.usend.at[c, d], f.urecv.at[c, d], to_up
+            )
+        return remote(
+            pick(f.acc), pick(f.dn), f.dsend.at[c, d], f.drecv.at[c, d], to_down
+        )
 
     def each_d(run, least=1):
         for k in range(last, least - 1, -1):
@@ -154,15 +172,27 @@
         turned = scaled.T
         for j in range(LANES // rows):
             b = i * (LANES // rows) + j
-            shalf[b % 2, b // 4, (b // 2) % 2] = turned[j * rows : (j + 1) * rows]
+            sall[node * near + b // 4, (b // 2) % 2, b % 2] = turned[j * rows : (j + 1) * rows]
     for i in range(near):
         x_scaled(i).start()
     for off in range(1, nodes):
         swap_turned(off).start()
         swap_scaled(off).start()
     lax.fori_loop(1, chunks, lambda c, carry: (x_hidden(c).start(), carry)[1], 0)
-    for i in range(near):
-        scat[node * near + i, :, :, :slots] = shalf[mx, i]
+    for off in range(1, nodes):
+        swap_turned(off).wait_recv()
+
+    def make_lone(d, carry):
+        part = sall[d].reshape(4 * rows, slots)
+        units = hid[:slots, columns(chunks)]
+        product = jnp.dot(part, units, preferred_element_type=F32).astype(BF16)
+        qacc[0, d] = product.reshape(2, 2 * rows, WIDE)
+        scat[d, :, :, :slots] = sall[d, :, mx]
+        return carry
+
+    lax.fori_loop(0, depth, make_lone, 0)
+    each_d(lambda d, k: y_copy(lone, 0, d).start())
+    y_copy(lone, 0, mz).start()
     for off in range(1, nodes):
         swap_scaled(off).wait_recv()
 
@@ -170,7 +200,7 @@
         slot = c % 2
         w_copy(c, slot).wait()
 
-        @pl.when(c + 1 < chunks)
+        @pl.when(c + 1 < total_chunks)
         def _():
             w_copy(c + 1, 1 - slot).start()
 
@@ -189,7 +219,7 @@
 
         @pl.when((k > 1) | ((k == 1) & jnp.logical_not(late(c))))
         def _():
-            y_copy(c, d).start()
+            y_copy(main, c, d).start()
 
     def make_first(owner, i):
         d = owner * near + nth(owner, i)
@@ -198,14 +228,73 @@
         acc[0, d] = product.reshape(2, rows, WIDE)
         send(0, d)
 
+    def single(f, c, d, rising):
+        inside = not_first if rising else not_last
+        into = f.up if rising else f.dn
+        y_copy(f, c, d).wait_recv()
+
+        @pl.when(inside)
+        def _():
+            z_copy(f, c, d, rising, False).wait_recv()
+            f.acc[c, d, my] = added(f.acc[c, d, my], f.ry[c, d], into[c, d, my])
+
+        @pl.when(jnp.logical_not(inside))
+        def _():
+            f.acc[c, d, my] = added(f.acc[c, d, my], f.ry[c, d])
+
+        z_copy(f, c, d, rising, False).start()
+
+    def pass_on(f, c, rising, first=None, least=2):
+        for k in range(first or last, least - 1, -1):
+            d = mz + k if rising else mz - k
+
+            @pl.when((d <= last) if rising else (d >= 0))
+            def _():
+                single(f, c, d, rising)
+
+    def hand_over(f, c, rising):
+        inside = not_first if rising else not_last
+        into = f.up if rising else f.dn
+        d = mz + 1 if rising else mz - 1
+
+        @pl.when(f.late(c))
+        def _():
+            @pl.when(inside)
+            def _():
+                z_copy(f, c, d, rising, False).wait_recv()
+                f.acc[c, d, my] = added(f.acc[c, d, my], into[c, d, my])
+
+            z_copy(f, c, d, rising, True).start()
+
+        @pl.when(jnp.logical_not(f.late(c)))
+        def _():
+            single(f, c, d, rising)
+
+    def at_ends(run):
+        @pl.when(mz == 0)
+        def _():
+            run(True)
+
+        @pl.when(mz == last)
+        def _():
+            run(False)
+
     done = 0
-    for i in range(near):
-        until = chunks * (i + near) // (2 * near)
+
+    def hidden_until(share):
+        nonlocal done
+        until = total_chunks * share // 14
         hidden_range(done, until)
         done = until
-        if i == 0:
-            for off in range(1, nodes):
-                swap_turned(off).wait_recv()
+
+    hidden_until(5)
+    at_ends(lambda rising: pass_on(lone, 0, rising, last, last))
+    hidden_until(7)
+    at_ends(lambda rising: pass_on(lone, 0, rising, last - 1, 2))
+    for i in range(near):
+        if i == 1:
+            hidden_until(9)
+            at_ends(lambda rising: hand_over(lone, 0, rising))
         x_scaled(i).wait_recv()
         for off in range(1, nodes):
             forward(off, i).start()
@@ -215,6 +304,8 @@
         for off in range(1, nodes):
             forward(off, i).wait_recv()
             make_first((node + nodes - off) % nodes, i)
+    if near == 1:
+        at_ends(lambda rising: hand_over(lone, 0, rising))
 
     def make(c):
         x_hidden(c).wait_recv()
@@ -228,80 +319,25 @@
 
         lax.fori_loop(0, depth // 2, two, 0)
 
-        @pl.when(late(c) & (c < EARLY))
-        def _():
-            @pl.when(mz == 0)
-            def _():
-                hand_over(c, True)
-
-            @pl.when(mz == last)
-            def _():
-                hand_over(c, False)
-
         each_d(lambda d, k: send(c, d))
-
-    def pass_on(c, rising):
-        inside = not_first if rising else not_last
-        into = up if rising else dn
-
-        def single(d):
-            y_copy(c, d).wait_recv()
-
-            @pl.when(inside)
-            def _():
-                z_copy(c, d, rising, False).wait_recv()
-                acc[c, d, my] = added(acc[c, d, my], ry[c, d], into[c, d, my])
-
-            @pl.when(jnp.logical_not(inside))
-            def _():
-                acc[c, d, my] = added(acc[c, d, my], ry[c, d])
-
-            z_copy(c, d, rising, False).start()
-
-        for k in range(last, 1, -1):
-            d = mz + k if rising else mz - k
-
-            @pl.when((d <= last) if rising else (d >= 0))
-            def _():
-                single(d)
-
-    def hand_over(c, rising):
-        inside = not_first if rising else not_last
-        into = up if rising else dn
-        d = mz + 1 if rising else mz - 1
-
-        @pl.when(inside)
-        def _():
-            z_copy(c, d, rising, False).wait_recv()
-            acc[c, d, my] = added(acc[c, d, my], into[c, d, my])
-
-        @pl.when(late(c))
-        def _():
-            z_copy(c, d, rising, True).start()
-
-        @pl.when(jnp.logical_not(late(c)))
-        def _():
-            y_copy(c, d).wait_recv()
-            acc[c, d, my] = added(acc[c, d, my], ry[c, d])
-            z_copy(c, d, rising, False).start()
 
     def settle(c):
         @pl.when(late(c))
         def _():
             @pl.when(not_first)
             def _():
-                z_copy(c, mz, True, True).wait_recv()
+                z_copy(main, c, mz, True, True).wait_recv()
                 acc[c, mz] = added(acc[c, mz], up[c, mz])
 
             @pl.when(not_last)
             def _():
-                z_copy(c, mz, False, True).wait_recv()
+                z_copy(main, c, mz, False, True).wait_recv()
                 acc[c, mz] = added(acc[c, mz], dn[c, mz])
 
-            y_copy(c, mz).start()
+            y_copy(main, c, mz).start()
 
     def finish(c):
-        y_copy(c, mz).wait_recv()
+        y_copy(main, c, mz).wait_recv()
         cols = columns(c)
 
         @pl.when(late(c))
@@ -312,11 +348,11 @@
         def _():
             @pl.when(not_first)
             def _():
-                z_copy(c, mz, True, False).wait_recv()
+                z_copy(main, c, mz, True, False).wait_recv()
 
             @pl.when(not_last)
             def _():
-                z_copy(c, mz, False, False).wait_recv()
+                z_copy(main, c, mz, False, False).wait_recv()
 
             @pl.when(mz == 0)
             def _():
@@ -337,49 +373,100 @@
         def _():
             run(c)
 
-    settled = AHEAD + HOP * last + DEFER + 1
+    def finish_lone():
+        y_copy(lone, 0, mz).wait_recv()
+
+        @pl.when(not_first)
+        def _():
+            z_copy(lone, 0, mz, True, False).wait_recv()
+
+        @pl.when(not_last)
+        def _():
+            z_copy(lone, 0, mz, False, False).wait_recv()
+
+        own_part, across = qacc[0, mz, my], qry[0, mz]
+
+        @pl.when(mz == 0)
+        def _():
+            qacc[0, mz, my] = added(own_part, across, qdn[0, mz, my])
+
+        @pl.when(mz == last)
+        def _():
+            qacc[0, mz, my] = added(own_part, across, qup[0, mz, my])
+
+        @pl.when(not_first & not_last)
+        def _():
+            qacc[0, mz, my] = added(own_part, across, qup[0, mz, my], qdn[0, mz, my])
+
+        x_lone().start()
+
+    def x_lone():
+        src = qacc.at[0, mz, my, pl.ds(pl.multiple_of(px * rows, rows), rows)]
+        return remote(src, qrx, qxsend, qxrecv, to_x)
+
+    settled = AHEAD + HOP * last + DEFER
+    below, above = mz, last - mz
+
+    def turn(dist):
+        return dist - 1 + jnp.minimum(dist - 1, 1)
+
+    finished = last + 3
 
     def step(t, carry):
         @pl.when((t > 0) & (t < chunks))
         def _():
             make(t)
 
-        @pl.when(t + done < chunks)
+        @pl.when((t >= NEAR) & (t < chunks + NEAR) & jnp.logical_not(late(t - NEAR)))
+        def _():
+            y_copy(main, t - NEAR, mz).start()
+
+        rise = t - AHEAD - HOP * below
+        fall = t - AHEAD - HOP * above
+
+        @pl.when(not_last)
+        def _():
+            within(rise, lambda c: pass_on(main, c, True))
+
+            @pl.when(not_first & (t == turn(below)))
+            def _():
+                pass_on(lone, 0, True, None, 1)
+
+        @pl.when(not_first)
+        def _():
+            within(fall, lambda c: pass_on(main, c, False))
+
+            @pl.when(not_last & (t == turn(above)))
+            def _():
+                pass_on(lone, 0, False, None, 1)
+
+        @pl.when(t + done < total_chunks)
         def _():
             make_hidden(t + done)
 
-        rise = t - AHEAD - HOP * mz
-        fall = t - AHEAD - HOP * (last - mz)
-
         @pl.when(not_last)
         def _():
-            within(rise, lambda c: pass_on(c, True))
+            within(rise - DEFER, lambda c: hand_over(main, c, True))
 
         @pl.when(not_first)
         def _():
-            within(fall, lambda c: pass_on(c, False))
-
-        def early(c, inside):
-            return late(c) & (c < EARLY) & jnp.logical_not(inside)
-
-        @pl.when(not_last & jnp.logical_not(early(rise - DEFER, not_first)))
-        def _():
-            within(rise - DEFER, lambda c: hand_over(c, True))
-
-        @pl.when(not_first & jnp.logical_not(early(fall - DEFER, not_last)))
-        def _():
-            within(fall - DEFER, lambda c: hand_over(c, False))
+            within(fall - DEFER, lambda c: hand_over(main, c, False))
 
         within(t - settled, settle)
-
-        @pl.when((t >= NEAR) & (t < chunks + NEAR) & jnp.logical_not(late(t - NEAR)))
-        def _():
-            y_copy(t - NEAR, mz).start()
-
-        within(t - settled - 2, finish)
+        within(t - settled - LAST, finish)
+
+        @pl.when(t == finished)
+        def _():
+            finish_lone()
+
         return carry
 
-    lax.fori_loop(0, chunks + settled + 2, step, 0)
+    steps = max(chunks + settled + LAST, total_chunks - done, finished + 1)
+    lax.fori_loop(0, steps, step, 0)
+    x_lone().wait_recv()
+    mine = pl.ds(pl.multiple_of(mx * rows, rows), rows)
+    gw_ref[:, columns(chunks)] = added(qacc[0, mz, my, mine], qrx[...])
+    x_lone().wait_send()
 
     for off in range(1, nodes):
         swap_turned(off).wait_send()
@@ -389,17 +476,16 @@
     for i in range(near):
         x_scaled(i).wait_send()
 
-    def drain(c, carry):
-        x_hidden(c).wait_send()
-        y_copy(c, mz).wait_send()
+    def drain(f, c):
+        y_copy(f, c, mz).wait_send()
 
         def one(d, k):
             if k > 1:
-                y_copy(c, d).wait_send()
+                y_copy(f, c, d).wait_send()
             else:
-                @pl.when(jnp.logical_not(late(c)))
+                @pl.when(jnp.logical_not(f.late(c)))
                 def _():
-                    y_copy(c, d).wait_send()
+                    y_copy(f, c, d).wait_send()
 
         each_d(one)
         for k in range(1, depth):
@@ -409,18 +495,23 @@
                 @pl.when((d <= last) if rising else (d >= 0))
                 def _():
                     if k > 1:
-                        z_copy(c, d, rising, False).wait_send()
+                        z_copy(f, c, d, rising, False).wait_send()
                     else:
-                        @pl.when(late(c))
+                        @pl.when(f.late(c))
                         def _():
-                            z_copy(c, d, rising, True).wait_send()
-
-                        @pl.when(jnp.logical_not(late(c)))
+                            z_copy(f, c, d, rising, True).wait_send()
+
+                        @pl.when(jnp.logical_not(f.late(c)))
                         def _():
-                            z_copy(c, d, rising, False).wait_send()
+                            z_copy(f, c, d, rising, False).wait_send()
+
+    def drain_main(c, carry):
+        x_hidden(c).wait_send()
+        drain(main, c)
         return carry
 
-    lax.fori_loop(0, chunks, drain, 0)
+    lax.fori_loop(0, chunks, drain_main, 0)
+    drain(lone, 0)
 
 
 def body(grad_out, gate_prob, hidden, w_down, slot_counts):
@@ -451,14 +542,19 @@
         scratch_shapes=[
             pltpu.VMEM((slots, half), BF16),
             pltpu.VMEM((nodes, slots, half), BF16),
-            pltpu.VMEM((2, near, 2, rows, slots), BF16),
+            pltpu.VMEM((depth, 2, 2, rows, slots), BF16),
             pltpu.VMEM((depth, 2, rows, 2 * slots), BF16),
             pltpu.VMEM((2 * slots, chunks * WIDE), BF16),
             pltpu.VMEM((2, model, WIDE), BF16),
-            pltpu.VMEM((chunks, depth, 2, rows, WIDE), BF16),
-            pltpu.VMEM((chunks, depth, rows, WIDE), BF16),
-            pltpu.VMEM((chunks, depth, 2, rows, WIDE), BF16),
-            pltpu.VMEM((chunks, depth, 2, rows, WIDE), BF16),
+            pltpu.VMEM((chunks - 1, depth, 2, rows, WIDE), BF16),
+            pltpu.VMEM((chunks - 1, depth, rows, WIDE), BF16),
+            pltpu.VMEM((chunks - 1, depth, 2, rows, WIDE), BF16),
+            pltpu.VMEM((chunks - 1, depth, 2, rows, WIDE), BF16),
+            pltpu.VMEM((1, depth, 2, 2 * rows, WIDE), BF16),
+            pltpu.VMEM((1, depth, 2 * rows, WIDE), BF16),
+            pltpu.VMEM((1, depth, 2, 2 * rows, WIDE), BF16),
+            pltpu.VMEM((1, depth, 2, 2 * rows, WIDE), BF16),
+            pltpu.VMEM((rows, WIDE), BF16),
             dma(()),
             dma(()),
             dma((2,)),
@@ -478,7 +574,9 @@
             dma((chunks, depth)),
             dma((chunks, depth)),
             dma((chunks, depth)),
-        ],
+        ]
+        + [dma((1, depth))] * 6
+        + [dma(())] * 2,
         compiler_params=pltpu.CompilerParams(
             collective_id=0, has_side_effects=True, vmem_limit_bytes=54 * 1024 * 1024
         ),

time: 106 us -> 102 us (0.962)
  Pallas kernels: 102 us -> 97.6 us
    pallas_call x1, Pallas kernels: 102 us -> 97.6 us  [body(): pl.pallas_call(functools.partial(kernel, (nodes, depth, chunks)), out_sha...]
where the time goes in v3:
time: 102 us; the launch traced here: 101 us
  Pallas kernels  97.6 us (96%)
  local copies, waits for them, and re-layouts  2.46 us (2%)
  between operations  1.29 us (1%)
    pallas_call x1, Pallas kernels, body(): pl.pallas_call(functools.partial(kernel, (nodes, depth, chunks)), out_sha...  97.6 us
    unnamed x2, local copies, waits for them, and re-layouts  2.46 us

profile of v3, /device:TPU:0, one launch (start us, length us, event | category | flops | bytes accessed | tf_op | source)
XLA Modules:
  0.0 101.4 jit_solution(6477575417737990618)
XLA Ops:
  1.3 97.6 %shard_map.68 = (bf16[384,3584]{1,0:T(8,128)(2,1)S(1)}, bf16[128,3584]{1,0:T(8,128)(2,1)S(1)}) custom-call(bf16[384,1024]{1,0:T(8,128)(2,1)} %go_any.1, f32[384]{0:T(512)} %gate_ref.1, s32[1]{0:T(128)S(6)} %copy.11.count_ref, bf16[384,3584]{1,0:T(8,128)(2,1)} %hid_any.1, bf16[2048,3584]{1,0:T(8,128)(2,1)} %w_ref.1), custom_call_target="tpu_custom_call" | custom-call | tf_op jit(solution)/shard_map/pallas_call | solution.py:534
  98.9 1.5 %copy.9 = bf16[384,3584]{1,0:T(8,128)(2,1)} copy(bf16[384,3584]{1,0:T(8,128)(2,1)S(1)} %get-tuple-element.2) | data formatting | bytes 5505024
  100.4 0.9 copy.10

commit v4 on v3

--- a/solution.py
+++ b/solution.py
@@ -16,6 +16,7 @@
 DEFER = 1
 NEAR = 3
 LAST = 3
+SHARES = (3, 5, 7, 9)
 F32, BF16 = jnp.float32, jnp.bfloat16
 
 
@@ -27,8 +28,8 @@
 
 
 def kernel(
-    dims, go_any, gate_ref, count_ref, hid_any, w_ref, gh_ref, gw_ref,
-    go, g, sall, scat, hid, wbuf, acc, ry, up, dn, qacc, qry, qup, qdn, qrx,
+    dims, go_any, gate_any, count_any, hid_any, w_ref, gh_ref, gw_ref,
+    gate_ref, count_ref, go, g, sall, scat, hid, wbuf, acc, ry, up, dn, qacc, qry, qup, qdn, qrx,
     gosem, hsem, wsem, gsend, grecv, ssend, srecv, xsend, xrecv, fsend, frecv,
     hsend, hrecv, ysend, yrecv, usend, urecv, dsend, drecv,
     qysend, qyrecv, qusend, qurecv, qdsend, qdrecv, qxsend, qxrecv,
@@ -49,6 +50,28 @@
     to_y = {"grp": me + 2 - 4 * my}
     to_up, to_down = {"grp": me + 4}, {"grp": me - 4}
 
+    def columns(c):
+        return pl.ds(pl.multiple_of(c * WIDE, WIDE), WIDE)
+
+    def w_copy(c, slot):
+        return pltpu.make_async_copy(w_ref.at[:, columns(c)], wbuf.at[slot], wsem.at[slot])
+
+    own = pl.ds(0, slots)
+    theirs = pl.ds(slots, slots)
+    first, rest, final = pl.ds(0, WIDE), pl.ds(WIDE, (chunks - 1) * WIDE), columns(chunks)
+
+    def take(cols, i):
+        return pltpu.make_async_copy(hid_any.at[:, cols], hid.at[own, cols], hsem.at[i])
+
+    take_grad = pltpu.make_async_copy(go_any, go, gosem.at[0])
+    take_gate = pltpu.make_async_copy(gate_any, gate_ref, gosem.at[1])
+    take_count = pltpu.make_async_copy(count_any, count_ref, gosem.at[2])
+    take_count.start()
+    take_gate.start()
+    take_grad.start()
+    take(first, 0).start()
+    take(final, 1).start()
+
     barrier = pltpu.get_barrier_semaphore()
 
     def greet(target):
@@ -66,20 +89,6 @@
     @pl.when(not_last)
     def _():
         greet(to_up)
-
-    def columns(c):
-        return pl.ds(pl.multiple_of(c * WIDE, WIDE), WIDE)
-
-    def w_copy(c, slot):
-        return pltpu.make_async_copy(w_ref.at[:, columns(c)], wbuf.at[slot], wsem.at[slot])
-
-    own = pl.ds(0, slots)
-    theirs = pl.ds(slots, slots)
-    take_hidden = pltpu.make_async_copy(hid_any, hid.at[own], hsem)
-    take_grad = pltpu.make_async_copy(go_any, go, gosem)
-    take_grad.start()
-    take_hidden.start()
-    w_copy(0, 0).start()
 
     def remote(src, dst, ssem, rsem, target):
         return pltpu.make_async_remote_copy(
@@ -155,12 +164,11 @@
             def _():
                 run(mz - k, k)
 
-    pl.semaphore_wait(
-        barrier, 1 + nodes + not_first.astype(jnp.int32) + not_last.astype(jnp.int32)
-    )
-    take_hidden.wait()
-    x_hidden(0).start()
+    take_count.wait()
+    take_gate.wait()
     take_grad.wait()
+    take(rest, 2).start()
+    w_copy(0, 0).start()
 
     live = lax.broadcasted_iota(jnp.int32, (LANES, slots), 1) < count_ref[0]
     gate = jnp.broadcast_to(gate_ref[...].reshape(1, slots), (LANES, slots))
@@ -173,25 +181,47 @@
         for j in range(LANES // rows):
             b = i * (LANES // rows) + j
             sall[node * near + b // 4, (b // 2) % 2, b % 2] = turned[j * rows : (j + 1) * rows]
+    pl.semaphore_wait(
+        barrier, 1 + nodes + not_first.astype(jnp.int32) + not_last.astype(jnp.int32)
+    )
+    take(first, 0).wait()
+    x_hidden(0).start()
     for i in range(near):
         x_scaled(i).start()
     for off in range(1, nodes):
         swap_turned(off).start()
+    for off in range(1, nodes):
         swap_scaled(off).start()
-    lax.fori_loop(1, chunks, lambda c, carry: (x_hidden(c).start(), carry)[1], 0)
-    for off in range(1, nodes):
-        swap_turned(off).wait_recv()
-
-    def make_lone(d, carry):
+    take(final, 1).wait()
+
+    def lone_row(j):
+        i = j % near
+        i = jnp.where(2 * mz < depth, near - 1 - i, i)
+        return (node + nodes - j // near) % nodes * near + i
+
+    def make_lone(j, carry):
+        d = lone_row(j)
         part = sall[d].reshape(4 * rows, slots)
         units = hid[:slots, columns(chunks)]
         product = jnp.dot(part, units, preferred_element_type=F32).astype(BF16)
         qacc[0, d] = product.reshape(2, 2 * rows, WIDE)
+
+        @pl.when(d != mz)
+        def _():
+            y_copy(lone, 0, d).start()
+
         scat[d, :, :, :slots] = sall[d, :, mx]
         return carry
 
-    lax.fori_loop(0, depth, make_lone, 0)
-    each_d(lambda d, k: y_copy(lone, 0, d).start())
+    def lone_rows(off):
+        lax.fori_loop(off * near, off * near + near, make_lone, 0)
+
+    lone_rows(0)
+    take(rest, 2).wait()
+    lax.fori_loop(1, chunks, lambda c, carry: (x_hidden(c).start(), carry)[1], 0)
+    for off in range(1, nodes):
+        swap_turned(off).wait_recv()
+        lone_rows(off)
     y_copy(lone, 0, mz).start()
     for off in range(1, nodes):
         swap_scaled(off).wait_recv()
@@ -287,14 +317,26 @@
         hidden_range(done, until)
         done = until
 
-    hidden_until(5)
-    at_ends(lambda rising: pass_on(lone, 0, rising, last, last))
-    hidden_until(7)
-    at_ends(lambda rising: pass_on(lone, 0, rising, last - 1, 2))
+    def lone_pass(start, stop):
+        def one(j, carry):
+            @pl.when(lone_row(j) != mz)
+            def _():
+                at_ends(lambda rising: single(lone, 0, lone_row(j), rising))
+
+            return carry
+
+        lax.fori_loop(start, stop, one, 0)
+
+    hidden_until(SHARES[0])
+    lone_pass(0, 1)
+    hidden_until(SHARES[1])
+    lone_pass(1, 2)
+    hidden_until(SHARES[2])
+    lone_pass(2, 3)
     for i in range(near):
-        if i == 1:
-            hidden_until(9)
-            at_ends(lambda rising: hand_over(lone, 0, rising))
+        if i == near - 1:
+            hidden_until(SHARES[3])
+            lone_pass(3, depth)
         x_scaled(i).wait_recv()
         for off in range(1, nodes):
             forward(off, i).start()
@@ -304,9 +346,6 @@
         for off in range(1, nodes):
             forward(off, i).wait_recv()
             make_first((node + nodes - off) % nodes, i)
-    if near == 1:
-        at_ends(lambda rising: hand_over(lone, 0, rising))
-
     def make(c):
         x_hidden(c).wait_recv()
         units = hid[:, columns(c)]
@@ -403,78 +442,6 @@
     def x_lone():
         src = qacc.at[0, mz, my, pl.ds(pl.multiple_of(px * rows, rows), rows)]
         return remote(src, qrx, qxsend, qxrecv, to_x)
-
-    settled = AHEAD + HOP * last + DEFER
-    below, above = mz, last - mz
-
-    def turn(dist):
-        return dist - 1 + jnp.minimum(dist - 1, 1)
-
-    finished = last + 3
-
-    def step(t, carry):
-        @pl.when((t > 0) & (t < chunks))
-        def _():
-            make(t)
-
-        @pl.when((t >= NEAR) & (t < chunks + NEAR) & jnp.logical_not(late(t - NEAR)))
-        def _():
-            y_copy(main, t - NEAR, mz).start()
-
-        rise = t - AHEAD - HOP * below
-        fall = t - AHEAD - HOP * above
-
-        @pl.when(not_last)
-        def _():
-            within(rise, lambda c: pass_on(main, c, True))
-
-            @pl.when(not_first & (t == turn(below)))
-            def _():
-                pass_on(lone, 0, True, None, 1)
-
-        @pl.when(not_first)
-        def _():
-            within(fall, lambda c: pass_on(main, c, False))
-
-            @pl.when(not_last & (t == turn(above)))
-            def _():
-                pass_on(lone, 0, False, None, 1)
-
-        @pl.when(t + done < total_chunks)
-        def _():
-            make_hidden(t + done)
-
-        @pl.when(not_last)
-        def _():
-            within(rise - DEFER, lambda c: hand_over(main, c, True))
-
-        @pl.when(not_first)
-        def _():
-            within(fall - DEFER, lambda c: hand_over(main, c, False))
-
-        within(t - settled, settle)
-        within(t - settled - LAST, finish)
-
-        @pl.when(t == finished)
-        def _():
-            finish_lone()
-
-        return carry
-
-    steps = max(chunks + settled + LAST, total_chunks - done, finished + 1)
-    lax.fori_loop(0, steps, step, 0)
-    x_lone().wait_recv()
-    mine = pl.ds(pl.multiple_of(mx * rows, rows), rows)
-    gw_ref[:, columns(chunks)] = added(qacc[0, mz, my, mine], qrx[...])
-    x_lone().wait_send()
-
-    for off in range(1, nodes):
-        swap_turned(off).wait_send()
-        swap_scaled(off).wait_send()
-        for i in range(near):
-            forward(off, i).wait_send()
-    for i in range(near):
-        x_scaled(i).wait_send()
 
     def drain(f, c):
         y_copy(f, c, mz).wait_send()
@@ -505,14 +472,83 @@
                         def _():
                             z_copy(f, c, d, rising, False).wait_send()
 
-    def drain_main(c, carry):
-        x_hidden(c).wait_send()
-        drain(main, c)
+    settled = AHEAD + HOP * last + DEFER
+    below, above = mz, last - mz
+
+    def turn(dist):
+        return dist - 1 + jnp.minimum(dist - 1, 1)
+
+    finished = last + 3
+
+    def step(t, carry):
+        @pl.when((t > 0) & (t < chunks))
+        def _():
+            make(t)
+
+        @pl.when((t >= NEAR) & (t < chunks + NEAR) & jnp.logical_not(late(t - NEAR)))
+        def _():
+            y_copy(main, t - NEAR, mz).start()
+
+        rise = t - AHEAD - HOP * below
+        fall = t - AHEAD - HOP * above
+
+        @pl.when(not_last)
+        def _():
+            within(rise, lambda c: pass_on(main, c, True))
+
+            @pl.when(not_first & (t == turn(below)))
+            def _():
+                pass_on(lone, 0, True, None, 1)
+
+        @pl.when(not_first)
+        def _():
+            within(fall, lambda c: pass_on(main, c, False))
+
+            @pl.when(not_last & (t == turn(above)))
+            def _():
+                pass_on(lone, 0, False, None, 1)
+
+        @pl.when(t + done < total_chunks)
+        def _():
+            make_hidden(t + done)
+
+        @pl.when(not_last)
+        def _():
+            within(rise - DEFER, lambda c: hand_over(main, c, True))
+
+        @pl.when(not_first)
+        def _():
+            within(fall - DEFER, lambda c: hand_over(main, c, False))
+
+        within(t - settled, settle)
+        def close(c):
+            finish(c)
+            x_hidden(c).wait_send()
+            drain(main, c)
+
+        within(t - settled - LAST, close)
+
+        @pl.when(t == finished)
+        def _():
+            finish_lone()
+            drain(lone, 0)
+
         return carry
 
-    lax.fori_loop(0, chunks, drain_main, 0)
-    drain(lone, 0)
-
+    steps = max(chunks + settled + LAST, total_chunks - done, finished + 1)
+    lax.fori_loop(0, steps, step, 0)
+    x_lone().wait_recv()
+    mine = pl.ds(pl.multiple_of(mx * rows, rows), rows)
+    gw_ref[:, columns(chunks)] = added(qacc[0, mz, my, mine], qrx[...])
+    x_lone().wait_send()
+
+    for off in range(1, nodes):
+        swap_turned(off).wait_send()
+        swap_scaled(off).wait_send()
+        for i in range(near):
+            forward(off, i).wait_send()
+    for i in range(near):
+        x_scaled(i).wait_send()
 
 def body(grad_out, gate_prob, hidden, w_down, slot_counts):
     slots, half = grad_out.shape
@@ -529,17 +565,19 @@
         w_down = jnp.pad(w_down, ((0, 0), (0, extra)))
     dma = pltpu.SemaphoreType.DMA
     vmem = pl.BlockSpec(memory_space=pltpu.VMEM)
-    smem = pl.BlockSpec(memory_space=pltpu.SMEM)
     anywhere = pl.BlockSpec(memory_space=pl.ANY)
+    hbm = pl.BlockSpec(memory_space=pltpu.HBM)
     grad_hidden, grad_weight = pl.pallas_call(
         functools.partial(kernel, (nodes, depth, chunks)),
         out_shape=(
             pltpu.VMEM((slots, chunks * WIDE), BF16),
             pltpu.VMEM((rows, chunks * WIDE), BF16),
         ),
-        in_specs=[anywhere, vmem, smem, anywhere, anywhere],
+        in_specs=[anywhere, anywhere, hbm, anywhere, anywhere],
         out_specs=(vmem, vmem),
         scratch_shapes=[
+            pltpu.VMEM((slots,), F32),
+            pltpu.SMEM((1,), jnp.int32),
             pltpu.VMEM((slots, half), BF16),
             pltpu.VMEM((nodes, slots, half), BF16),
             pltpu.VMEM((depth, 2, 2, rows, slots), BF16),
@@ -555,8 +593,8 @@
             pltpu.VMEM((1, depth, 2, 2 * rows, WIDE), BF16),
             pltpu.VMEM((1, depth, 2, 2 * rows, WIDE), BF16),
             pltpu.VMEM((rows, WIDE), BF16),
-            dma(()),
-            dma(()),
+            dma((3,)),
+            dma((3,)),
             dma((2,)),
             dma((nodes,)),
             dma((nodes,)),

time: 102 us -> 99.9 us (0.979)
  Pallas kernels: 97.6 us -> 95.8 us
    pallas_call x1, Pallas kernels: 97.6 us -> 95.8 us  [body(): pl.pallas_call(functools.partial(kernel, (nodes, depth, chunks)), out_sha...]
where the time goes in v4:
time: 99.9 us; the launch traced here: 99.6 us
  Pallas kernels  95.8 us (96%)
  local copies, waits for them, and re-layouts  2.46 us (2%)
  between operations  1.29 us (1%)
    pallas_call x1, Pallas kernels, body(): pl.pallas_call(functools.partial(kernel, (nodes, depth, chunks)), out_sha...  95.8 us
    unnamed x2, local copies, waits for them, and re-layouts  2.46 us

profile of v4, /device:TPU:0, one launch (start us, length us, event | category | flops | bytes accessed | tf_op | source)
XLA Modules:
  0.0 99.6 jit_solution(2462895710803527168)
XLA Ops:
  1.3 95.8 %shard_map.68 = (bf16[384,3584]{1,0:T(8,128)(2,1)S(1)}, bf16[128,3584]{1,0:T(8,128)(2,1)S(1)}) custom-call(bf16[384,1024]{1,0:T(8,128)(2,1)} %go_any.1, f32[384]{0:T(512)} %gate_any.1, s32[1]{0:T(128)S(6)} %copy.11.count_any, bf16[384,3584]{1,0:T(8,128)(2,1)} %hid_any.1, bf16[2048,3584]{1,0:T(8,128)(2,1)} %w_ref.1), custom_call_target="tpu_custom_call" | custom-call | tf_op jit(solution)/shard_map/pallas_call | solution.py:570
  97.1 1.5 %copy.9 = bf16[384,3584]{1,0:T(8,128)(2,1)} copy(bf16[384,3584]{1,0:T(8,128)(2,1)S(1)} %get-tuple-element.2) | data formatting | bytes 5505024
  98.6 0.9 copy.10

commit v5 on v4

--- a/solution.py
+++ b/solution.py
@@ -16,7 +16,7 @@
 DEFER = 1
 NEAR = 3
 LAST = 3
-SHARES = (3, 5, 7, 9)
+SHARES = (3, 5, 8, 10)
 F32, BF16 = jnp.float32, jnp.bfloat16
 
 
@@ -107,7 +107,7 @@
         return remote(ref, ref, ssend.at[off], srecv.at[off], peer(off))
 
     def nth(owner, i):
-        return jnp.where(2 * owner < nodes, i, near - 1 - i)
+        return jnp.where(2 * mz < depth, near - 1 - i, i)
 
     def x_scaled(i):
         d = node * near + nth(node, i)
@@ -508,19 +508,19 @@
             def _():
                 pass_on(lone, 0, False, None, 1)
 
+        @pl.when(not_last)
+        def _():
+            within(rise - DEFER, lambda c: hand_over(main, c, True))
+
+        @pl.when(not_first)
+        def _():
+            within(fall - DEFER, lambda c: hand_over(main, c, False))
+
+        within(t - settled, settle)
         @pl.when(t + done < total_chunks)
         def _():
             make_hidden(t + done)
 
-        @pl.when(not_last)
-        def _():
-            within(rise - DEFER, lambda c: hand_over(main, c, True))
-
-        @pl.when(not_first)
-        def _():
-            within(fall - DEFER, lambda c: hand_over(main, c, False))
-
-        within(t - settled, settle)
         def close(c):
             finish(c)
             x_hidden(c).wait_send()
@@ -549,6 +549,21 @@
             forward(off, i).wait_send()
     for i in range(near):
         x_scaled(i).wait_send()
+
+def store(pieces, gh_ref, gw_ref, gh_any, gw_any, sems):
+    slots, units = gh_any.shape
+    rows, kept = slots // pieces, pl.ds(0, units)
+    copies = [pltpu.make_async_copy(gw_ref.at[:, kept], gw_any, sems.at[pieces])]
+    for i in range(pieces):
+        part = pl.ds(i * rows, rows)
+        copies.append(
+            pltpu.make_async_copy(gh_ref.at[part, kept], gh_any.at[part], sems.at[i])
+        )
+    for copy in copies:
+        copy.start()
+    for copy in copies:
+        copy.wait()
+
 
 def body(grad_out, gate_prob, hidden, w_down, slot_counts):
     slots, half = grad_out.shape
@@ -619,7 +634,17 @@
             collective_id=0, has_side_effects=True, vmem_limit_bytes=54 * 1024 * 1024
         ),
     )(grad_out, gate_prob, slot_counts, hidden, w_down)
-    return grad_hidden[:, :units], grad_weight[:, :units]
+    return pl.pallas_call(
+        functools.partial(store, 3),
+        out_shape=(
+            jax.ShapeDtypeStruct((slots, units), BF16),
+            jax.ShapeDtypeStruct((rows, units), BF16),
+        ),
+        in_specs=[anywhere, anywhere],
+        out_specs=(anywhere, anywhere),
+        scratch_shapes=[dma((4,))],
+        compiler_params=pltpu.CompilerParams(vmem_limit_bytes=8 * 1024 * 1024),
+    )(grad_hidden, grad_weight)
 
 
 def solution(mesh):

time: 99.9 us -> 99.4 us (level)
  local copies, waits for them, and re-layouts: 2.46 us -> 0 us
  Pallas kernels: 95.8 us -> 97.7 us
    unnamed x2 -> x0, local copies, waits for them, and re-layouts: 2.46 us -> none
    pallas_call x0 -> x1, Pallas kernels: none -> 1.86 us  [body(): pl.pallas_call(functools.partial(store, 3), out_shape=(jax.ShapeDtypeStru...]
where the time goes in v5:
time: 99.4 us; the launch traced here: 99 us
  Pallas kernels  97.7 us (98%)
  between operations  1.29 us (1%)
    pallas_call x1, Pallas kernels, body(): pl.pallas_call(functools.partial(kernel, (nodes, depth, chunks)), out_sha...  95.8 us

profile of v5, /device:TPU:0, one launch (start us, length us, event | category | flops | bytes accessed | tf_op | source)
XLA Modules:
  0.0 99.0 jit_solution(13605431792605999075)
XLA Ops:
  1.3 95.8 %shard_map.68 = (bf16[384,3584]{1,0:T(8,128)(2,1)S(1)}, bf16[128,3584]{1,0:T(8,128)(2,1)S(1)}) custom-call(bf16[384,1024]{1,0:T(8,128)(2,1)} %go_any.1, f32[384]{0:T(512)} %gate_any.1, s32[1]{0:T(128)S(6)} %copy.7.count_any, bf16[384,3584]{1,0:T(8,128)(2,1)} %hid_any.1, bf16[2048,3584]{1,0:T(8,128)(2,1)} %w_ref.1), custom_call_target="tpu_custom_call" | custom-call | tf_op jit(solution)/shard_map/pallas_call | solution.py:585
  97.1 1.9 %shard_map.69 = (bf16[384,3584]{1,0:T(8,128)(2,1)}, bf16[128,3584]{1,0:T(8,128)(2,1)}) custom-call(bf16[384,3584]{1,0:T(8,128)(2,1)S(1)} %get-tuple-element.4.gh_ref, bf16[128,3584]{1,0:T(8,128)(2,1)S(1)} %get-tuple-element.5.gw_ref), custom_call_target="tpu_custom_call" | custom-call | tf_op jit(solution)/shard_map/pallas_call | solution.py:637

commit v6 on v5

--- a/solution.py
+++ b/solution.py
@@ -14,9 +14,10 @@
 AHEAD = 1
 HOP = 1
 DEFER = 1
-NEAR = 3
+NEAR = 4
 LAST = 3
-SHARES = (3, 5, 8, 10)
+SLOTS = 4
+SHARES = (4, 8, 11, 14)
 F32, BF16 = jnp.float32, jnp.bfloat16
 
 
@@ -168,7 +169,8 @@
     take_gate.wait()
     take_grad.wait()
     take(rest, 2).start()
-    w_copy(0, 0).start()
+    for c in range(min(SLOTS - 1, total_chunks)):
+        w_copy(c, c).start()
 
     live = lax.broadcasted_iota(jnp.int32, (LANES, slots), 1) < count_ref[0]
     gate = jnp.broadcast_to(gate_ref[...].reshape(1, slots), (LANES, slots))
@@ -227,12 +229,12 @@
         swap_scaled(off).wait_recv()
 
     def make_hidden(c):
-        slot = c % 2
+        slot, ahead = c % SLOTS, c + SLOTS - 1
         w_copy(c, slot).wait()
 
-        @pl.when(c + 1 < total_chunks)
-        def _():
-            w_copy(c + 1, 1 - slot).start()
+        @pl.when(ahead < total_chunks)
+        def _():
+            w_copy(ahead, ahead % SLOTS).start()
 
         total = jnp.dot(g[0], wbuf[slot, :half, :], preferred_element_type=F32)
         for i in range(1, nodes):
@@ -598,7 +600,7 @@
             pltpu.VMEM((depth, 2, 2, rows, slots), BF16),
             pltpu.VMEM((depth, 2, rows, 2 * slots), BF16),
             pltpu.VMEM((2 * slots, chunks * WIDE), BF16),
-            pltpu.VMEM((2, model, WIDE), BF16),
+            pltpu.VMEM((SLOTS, model, WIDE), BF16),
             pltpu.VMEM((chunks - 1, depth, 2, rows, WIDE), BF16),
             pltpu.VMEM((chunks - 1, depth, rows, WIDE), BF16),
             pltpu.VMEM((chunks - 1, depth, 2, rows, WIDE), BF16),
@@ -610,7 +612,7 @@
             pltpu.VMEM((rows, WIDE), BF16),
             dma((3,)),
             dma((3,)),
-            dma((2,)),
+            dma((SLOTS,)),
             dma((nodes,)),
             dma((nodes,)),
             dma((nodes,)),

time: 99.4 us -> 98.9 us (level)
  no operation moved by 1% of the time
where the time goes in v6:
time: 98.9 us; the launch traced here: 98.8 us
  Pallas kernels  97.5 us (99%)
  between operations  1.29 us (1%)
    pallas_call x1, Pallas kernels, body(): pl.pallas_call(functools.partial(kernel, (nodes, depth, chunks)), out_sha...  95.6 us

profile of v6, /device:TPU:0, one launch (start us, length us, event | category | flops | bytes accessed | tf_op | source)
XLA Modules:
  0.0 98.8 jit_solution(2992831651029808138)
XLA Ops:
  1.3 95.6 %shard_map.68 = (bf16[384,3584]{1,0:T(8,128)(2,1)S(1)}, bf16[128,3584]{1,0:T(8,128)(2,1)S(1)}) custom-call(bf16[384,1024]{1,0:T(8,128)(2,1)} %go_any.1, f32[384]{0:T(512)} %gate_any.1, s32[1]{0:T(128)S(6)} %copy.7.count_any, bf16[384,3584]{1,0:T(8,128)(2,1)} %hid_any.1, bf16[2048,3584]{1,0:T(8,128)(2,1)} %w_ref.1), custom_call_target="tpu_custom_call" | custom-call | tf_op jit(solution)/shard_map/pallas_call | solution.py:587
  96.9 1.9 %shard_map.69 = (bf16[384,3584]{1,0:T(8,128)(2,1)}, bf16[128,3584]{1,0:T(8,128)(2,1)}) custom-call(bf16[384,3584]{1,0:T(8,128)(2,1)S(1)} %get-tuple-element.4.gh_ref, bf16[128,3584]{1,0:T(8,128)(2,1)S(1)} %get-tuple-element.5.gw_ref), custom_call_target="tpu_custom_call" | custom-call | tf_op jit(solution)/shard_map/pallas_call | solution.py:639
